TPU v7x, 32 devices: a whole 2x2x4 slice. The times are simulated.
32 devices in a mesh: dp: 8 (over z, x), feat: 4 (over y, core).
Axes of the slice: x: 2, y: 2, z: 4, core: 2. Of those that a mesh axis runs over, the one named last changes fastest.
Arguments:
- features: float32 [24576, 2048], P('dp', 'feat'), may hold values from -200 to 200
- gamma: float32 [2048], P('feat'), may hold values from 0.5 to 1.5
- beta: float32 [2048], P('feat'), may hold values from -3 to 3
- weight: bfloat16 [2048, 2048], P(None, 'feat'), may hold values from -0.125 to 0.125
- bias: float32 [2048], P('feat'), may hold values from -3 to 3
Outputs:
- activated: float32 [24576, 2048], P('dp', 'feat')
All inputs are finite; a program needn't handle non-finite values.
Results may differ from a plain program's by a relative error of at most 0.0026.
Values may be sent and summed in bfloat16 or wider, within the bound.
No kernel may reach another device: no remote copies, remote signals or barrier semaphores. Data moves between devices by JAX's collectives and lax.ppermute only.
A program may use at most 128 MiB of HBM per device.

v0:
```python
import jax
import jax.numpy as jnp
from jax import lax
from jax.sharding import PartitionSpec as P


def local(features, gamma, beta, weight, bias):
    rows = features.shape[0]
    total_rows = rows * lax.axis_size("dp")
    sums = lax.psum(jnp.sum(features, axis=0), "dp")
    mean = sums / total_rows
    centred_here = features - mean
    devs = lax.psum(jnp.sum(centred_here * centred_here, axis=0), "dp")
    var = devs / total_rows
    scale = gamma / jnp.sqrt(var + 1e-05)
    normed = ((features - mean) * scale + beta).astype(jnp.bfloat16)
    product = jnp.dot(
        lax.all_gather(normed, "feat", axis=1, tiled=True),
        weight,
        preferred_element_type=jnp.float32,
    )
    return jnp.maximum(product + bias, 0.0)


def solution(mesh):
    placed = (P("dp", "feat"), P("feat"), P("feat"), P(None, "feat"), P("feat"))
    return jax.shard_map(
        local, mesh=mesh, in_specs=placed, out_specs=P("dp", "feat"), check_vma=False
    )
```

profile of v0, /device:TPU:0, one launch (start us, length us, event | category | flops | bytes accessed | tf_op | source)
XLA Modules:
  0.0 158.3 jit_solution(14574581504709749969)
XLA Ops:
  6.5 0.0 copy-start
  6.5 0.0 copy-start.2
  6.5 0.0 copy-start.1
  6.5 0.0 all-gather.2.cloned.1.call-start
  6.5 3.4 %reduce_sum.18 = f32[512]{0:T(512)S(1)} reduce(f32[3072,512]{1,0:T(8,128)} %param.5, f32[]{:T(128)} %constant.3.clone.1), dimensions={0}, to_apply=%region_0.0 | reduce | flops 1572352 | bytes 6293508 | tf_op jit(solution)/shard_map/reduce_sum | solution.py:10
  9.9 23.1 %psum.14 = f32[512]{0:T(512)S(1)} all-reduce(f32[512]{0:T(512)S(1)} %reduce_sum.18), channel_id=1, replica_groups=mesh['dp'=8,'feat'=4] {'dp'}, use_global_device_ids=true, to_apply=%region_1.0 | all-reduce | flops 512 | bytes 4096 | tf_op jit(solution)/shard_map/psum | solution.py:10
  33.1 3.5 %multiply_reduce_fusion = f32[512]{0:T(512)S(1)} fusion(f32[3072,512]{1,0:T(8,128)} %param.5, f32[512]{0:T(512)S(1)} %broadcast_multiply_fusion), kind=kLoop, calls=%fused_computation.2 | loop fusion | flops 4718080 | bytes 6295552 | tf_op jit(solution)/shard_map/reduce_sum | solution.py:13
  36.6 17.1 %psum.15 = f32[512]{0:T(512)S(1)} all-reduce(f32[512]{0:T(512)S(1)} %multiply_reduce_fusion), channel_id=1, replica_groups=mesh['dp'=8,'feat'=4] {'dp'}, use_global_device_ids=true, to_apply=%region_3.0 | all-reduce | flops 512 | bytes 4096 | tf_op jit(solution)/shard_map/psum | solution.py:13
  53.7 0.0 copy-done.2
  53.7 0.0 copy-done.1
  53.7 0.0 copy-start.3
  53.7 5.4 %add_convert_fusion = bf16[3072,512]{1,0:T(8,128)(2,1)} fusion(f32[3072,512]{1,0:T(8,128)} %param.5, f32[512]{0:T(512)S(1)} %copy-done.1, f32[512]{0:T(512)S(1)} %rsqrt_multiply_fusion, f32[512]{0:T(512)S(1)} %broadcast_multiply_fusion), kind=kLoop, calls=%fused_computation.1 | loop fusion | flops 6291456 | bytes 9443328 | tf_op jit(solution)/shard_map/convert_element_type | solution.py:16
  59.1 0.0 all-gather.2.cloned.1.call-update
  59.1 81.0 %all-gather.2.cloned.1.call-done = bf16[3072,2048]{1,0:T(8,128)(2,1)} async-done(((bf16[3072,512]{1,0:T(8,128)(2,1)}), bf16[3072,2048]{1,0:T(8,128)(2,1)}) %all-gather.2.cloned.1.call-update) | async-done | bytes 12582928 | tf_op jit(solution)/shard_map/all_gather | solution.py:18
  140.1 0.0 copy-done
  140.1 0.0 copy-done.3
  140.1 11.3 %add_maximum_fusion = f32[3072,512]{1,0:T(8,128)} fusion(bf16[3072,2048]{1,0:T(8,128)(2,1)} %all-gather.2.cloned.1.call-done, bf16[2048,512]{1,0:T(8,128)(2,1)S(1)} %copy-done, f32[512]{0:T(512)S(1)} %copy-done.3), kind=kOutput, calls=%fused_computation | convolution fusion | flops 6445596672 | bytes 20973568 | tf_op jit(solution)/shard_map/dot_general | solution.py:17
  (2 shorter events, 0.0 us)
Async XLA Ops:
  6.5 133.6 %copy-start = (bf16[2048,512]{1,0:T(8,128)(2,1)S(1)}, bf16[2048,512]{1,0:T(8,128)(2,1)}, u32[]{:S(2)}) copy-start(bf16[2048,512]{1,0:T(8,128)(2,1)} %param.8) | copy-start | bytes 6291460
  6.5 47.2 %copy-start.2 = (f32[512]{0:T(512)S(1)}, f32[512]{0:T(512)}, u32[]{:S(2)}) copy-start(f32[512]{0:T(512)} %param.6) | copy-start | bytes 6148
  6.5 47.2 %copy-start.1 = (f32[512]{0:T(512)S(1)}, f32[512]{0:T(512)}, u32[]{:S(2)}) copy-start(f32[512]{0:T(512)} %param.7) | copy-start | bytes 6148
  6.5 133.6 %all-gather.2.cloned.1.call-start = ((), (), s32[]{:S(2)}) async-start(), calls=%async_computation | async-start | bytes 15728640 | tf_op jit(solution)/shard_map/all_gather | solution.py:18
  53.7 86.4 %copy-start.3 = (f32[512]{0:T(512)S(1)}, f32[512]{0:T(512)}, u32[]{:S(2)}) copy-start(f32[512]{0:T(512)} %param.9) | copy-start | bytes 6148
Sparse Core Ops, SparseCore 0:
  59.3 80.8 all-gather.1
where the time goes:
time: 159 us; the launch traced here: 158 us
  waiting for transfers between devices  81 us (51%)
  blocking collectives  40.2 us (25%)
  between operations  13.4 us (8%)
  other arithmetic  12.3 us (8%)
  matrix products  11.3 us (7%)
    all_gather x1, waiting for transfers between devices, local(): lax.all_gather(normed, 'feat', axis=1, tiled=True)  81 us
    psum x1, blocking collectives, local(): sums = lax.psum(jnp.sum(features, axis=0), 'dp')  23.1 us
    psum x1, blocking collectives, local(): devs = lax.psum(jnp.sum(centred_here * centred_here, axis=0), 'dp')  17.1 us
    dot_general x1, matrix products, local(): jnp.dot(lax.all_gather(normed, 'feat', axis=1, tiled=True), weight, prefe...  11.3 us
    convert_element_type x1, other arithmetic, local(): normed = ((features - mean) * scale + beta).astype(jnp.bfloat16)  5.36 us
    reduce_sum x1, other arithmetic, local(): devs = lax.psum(jnp.sum(centred_here * centred_here, axis=0), 'dp')  3.52 us
    reduce_sum x1, other arithmetic, local(): sums = lax.psum(jnp.sum(features, axis=0), 'dp')  3.4 us
  transfers between devices with their start and end apart: 1, of which 1 were waited for; matrix products, arithmetic and copies ran while one was open for 0% of the time, Pallas kernels for 0%

commit v1 on v0

v1 whole, which is shorter than its diff:
```python
import functools

import jax
import jax.numpy as jnp
from jax import lax
from jax.experimental import pallas as pl
from jax.experimental.pallas import tpu as pltpu
from jax.sharding import PartitionSpec as P


UNITS = 24
EARLY = (2, 8)
LATE = (6, 4, 3, 1)


def grant(kib):
    return pltpu.CompilerParams(vmem_limit_bytes=kib * 1024)


def block_of(first, count, most):
    per = min(count, most)
    while count % per or first % per:
        per -= 1
    return per


def centre_kernel(x_ref, sent_ref, mean_ref, dev_ref):
    b = pl.program_id(0)
    x = x_ref[...]
    mean = jnp.mean(x, axis=0, keepdims=True)
    d = x - mean
    sent_ref[...] = d.astype(jnp.bfloat16)
    mean_ref[pl.ds(b, 1), :] = mean
    dev_ref[pl.ds(b, 1), :] = jnp.sum(d * d, axis=0, keepdims=True)


def centre(features, first, count, unit):
    cols = features.shape[1]
    per = block_of(first, count, 4)
    blocks = count // per
    return pl.pallas_call(
        centre_kernel,
        grid=(blocks,),
        in_specs=[pl.BlockSpec((per * unit, cols), lambda b: (b + first // per, 0))],
        out_specs=[
            pl.BlockSpec((per * unit, cols), lambda b: (b, 0)),
            pl.BlockSpec((blocks, cols), lambda b: (0, 0)),
            pl.BlockSpec((blocks, cols), lambda b: (0, 0)),
        ],
        out_shape=[
            jax.ShapeDtypeStruct((count * unit, cols), jnp.bfloat16),
            jax.ShapeDtypeStruct((blocks, cols), jnp.float32),
            jax.ShapeDtypeStruct((blocks, cols), jnp.float32),
        ],
        compiler_params=grant(8192),
    )(features)


def moments_kernel(x_ref, *refs, sizes, rest):
    early, (total_ref, sum_ref, dev_ref) = refs[: 2 * len(sizes)], refs[2 * len(sizes) :]
    b = pl.program_id(0)
    pivot = early[0][0:1, :]
    d = x_ref[...] - pivot
    d = d.reshape(-1, 8, d.shape[1])

    @pl.when(b == 0)
    def _():
        sum_ref[...] = jnp.zeros_like(sum_ref)
        dev_ref[...] = jnp.zeros_like(dev_ref)

    sum_ref[...] += jnp.sum(d, axis=0)
    dev_ref[...] += jnp.sum(d * d, axis=0)

    @pl.when(b == pl.num_programs(0) - 1)
    def _():
        shift = jnp.sum(sum_ref[...], axis=0, keepdims=True) / rest
        dev = jnp.sum(dev_ref[...], axis=0, keepdims=True) - rest * (shift * shift)
        groups = [(rest, pivot + shift, dev)]
        for n, m, d in zip(sizes, early[::2], early[1::2]):
            for r in range(m.shape[0]):
                groups.append((n, m[r : r + 1, :], d[r : r + 1, :]))
        rows = sum(n for n, _, _ in groups)
        mean = sum(n * m for n, m, _ in groups) / rows
        dev = sum(d + n * ((m - mean) * (m - mean)) for n, m, d in groups)
        total_ref[0:1, :] = mean
        total_ref[1:2, :] = dev


def moments(features, first, count, unit, early, sizes):
    cols = features.shape[1]
    per = block_of(first, count, 4)
    flat = [a for pair in early for a in pair]
    return pl.pallas_call(
        functools.partial(moments_kernel, sizes=sizes, rest=count * unit),
        grid=(count // per,),
        in_specs=[pl.BlockSpec((per * unit, cols), lambda b: (b + first // per, 0))]
        + [pl.BlockSpec(a.shape, lambda b: (0, 0)) for a in flat],
        out_specs=pl.BlockSpec((2, cols), lambda b: (0, 0)),
        out_shape=jax.ShapeDtypeStruct((2, cols), jnp.float32),
        scratch_shapes=[pltpu.VMEM((8, cols), jnp.float32)] * 2,
        compiler_params=grant(8192),
    )(features, *flat)


def shard_order():
    feat = lax.axis_size("feat")
    me = lax.axis_index("feat")
    order = [me, me ^ 1]
    for s in range(2, feat, 2):
        source = (me - s) % feat
        order += [source, source ^ 1]
    return order


def layer_kernel(*refs, shards):
    xs = refs[:shards]
    w_ref, bias_ref = refs[shards : shards + 2]
    out_ref = refs[-1]
    cols = xs[0].shape[1]
    total = bias_ref[...]
    for x, shard in zip(xs, shard_order()):
        start = pl.multiple_of(shard * cols, cols)
        total = total + jnp.dot(x[...], w_ref[pl.ds(start, cols), :], preferred_element_type=jnp.float32)
    out_ref[...] = jnp.maximum(total, 0.0)


def layer(xs, weight, bias, out, first, rows, unit):
    shards = len(xs)
    count, cols = xs[0].shape
    width = weight.shape[1]
    block = block_of(first, count // unit, 4)
    offset = first // block
    block *= unit
    in_specs = [pl.BlockSpec((block, cols), lambda i: (i, 0)) for _ in range(shards)]
    in_specs += [pl.BlockSpec(memory_space=pltpu.VMEM)] * 2
    args = [*xs, weight, bias]
    aliases = {}
    if out is not None:
        in_specs += [pl.BlockSpec(memory_space=pl.ANY)]
        aliases = {len(args): 0}
        args += [out]
    return pl.pallas_call(
        functools.partial(layer_kernel, shards=shards),
        grid=(count // block,),
        in_specs=in_specs,
        out_specs=pl.BlockSpec((block, width), lambda i: (i + offset, 0)),
        out_shape=jax.ShapeDtypeStruct((rows, width), jnp.float32),
        input_output_aliases=aliases,
        compiler_params=grant(12288),
    )(*args)


def local(features, gamma, beta, weight, bias):
    rows, cols = features.shape
    dp = lax.axis_size("dp")
    feat = lax.axis_size("feat")
    unit = rows // UNITS
    total_rows = rows * dp
    near = [(i, i ^ 1) for i in range(feat)]
    shifts = range(2, feat, 2)

    def to_far(x):
        return [lax.ppermute(x, "feat", [(i, (i + s) % feat) for i in range(feat)]) for s in shifts]

    def to_near(x):
        return lax.ppermute(x, "feat", near)

    early, found, sizes, firsts = [], [], [], [0]
    for count in EARLY + LATE:
        firsts.append(firsts[-1] + count)
    for k, count in enumerate(EARLY):
        sent, mean, dev = centre(features, firsts[k], count, unit)
        early.append(to_far(sent))
        found.append((mean, dev))
        sizes.append(count * unit // mean.shape[0])
    ahead = firsts[len(EARLY)]
    mine = moments(features, ahead, UNITS - ahead, unit, found, tuple(sizes))
    step, held = 1, rows
    while step < dp:
        theirs = lax.ppermute(mine, "dp", [(i, i ^ step) for i in range(dp)])
        gap = mine[0] - theirs[0]
        mean = (mine[0] + theirs[0]) * 0.5
        dev = mine[1] + theirs[1] + (0.5 * held) * (gap * gap)
        mine = jnp.stack([mean, dev])
        step, held = 2 * step, 2 * held
    mean = mine[0]
    var = mine[1] / total_rows
    scale = gamma / jnp.sqrt(var + 1e-05)

    def normalize(k):
        x = features[firsts[k] * unit : firsts[k + 1] * unit]
        return ((x - mean) * scale + beta).astype(jnp.bfloat16)

    own, arrived = {}, {}
    for k in range(len(EARLY), len(EARLY) + len(LATE)):
        own[k] = normalize(k)
        arrived[k] = to_far(own[k])
    offsets = (jnp.concatenate([m for m, _ in found]) - mean) * scale + beta
    table = to_far(jnp.concatenate([scale[None], offsets]))
    row = 1
    for k, (mean_of, _) in enumerate(found):
        own[k] = normalize(k)
        arrived[k] = []
        blocks = mean_of.shape[0]
        for got, t in zip(early[k], table):
            got = got.reshape(blocks, sizes[k], cols).astype(jnp.float32)
            got = got * t[0] + t[row : row + blocks][:, None, :]
            arrived[k].append(got.astype(jnp.bfloat16).reshape(blocks * sizes[k], cols))
        row += blocks

    out = None
    for k in range(len(EARLY) + len(LATE)):
        xs = [own[k], to_near(own[k])]
        for got in arrived[k]:
            xs += [got, to_near(got)]
        out = layer(xs, weight, bias[None], out, firsts[k], rows, unit)
    return out


def solution(mesh):
    placed = (P("dp", "feat"), P("feat"), P("feat"), P(None, "feat"), P("feat"))
    return jax.shard_map(
        local, mesh=mesh, in_specs=placed, out_specs=P("dp", "feat"), check_vma=False
    )
```

time: 159 us -> 101 us (0.64)
  blocking collectives: 40.2 us -> 0 us
  starting transfers between devices: 0.01 us -> 18.5 us
  waiting for transfers between devices: 81 us -> 62.7 us
  Pallas kernels: 0 us -> 15.4 us
  between operations: 13.4 us -> 0.24 us
  matrix products: 11.3 us -> 0 us
  other arithmetic: 12.3 us -> 1.34 us
  local copies, waits for them, and re-layouts: 0.02 us -> 2.83 us
    all_gather x1 -> x0, waiting for transfers between devices: 81 us -> none  [local(): lax.all_gather(normed, 'feat', axis=1, tiled=True)]
    ppermute x0 -> x22, waiting for transfers between devices: none -> 62.7 us  [the longest x7 56.9 us: to_far(): lax.ppermute(x, 'feat', [(i, (i + s) % feat) for i in range(feat)])]
    psum x2 -> x0, blocking collectives: 40.2 us -> none  [the longest x1 23.1 us: local(): sums = lax.psum(jnp.sum(features, axis=0), 'dp')]
    ppermute x0 -> x22, starting transfers between devices: none -> 18.5 us  [the longest x3 8.3 us: local(): theirs = lax.ppermute(mine, 'dp', [(i, i ^ step) for i in range(dp)])]
    pallas_call x0 -> x9, Pallas kernels: none -> 15.4 us  [the longest x6 13.9 us: layer(): pl.pallas_call(functools.partial(layer_kernel, shards=shards), grid=(coun...]
    dot_general x1 -> x0, matrix products: 11.3 us -> none  [local(): jnp.dot(lax.all_gather(normed, 'feat', axis=1, tiled=True), weight, prefe...]
    reduce_sum x2 -> x0, other arithmetic: 6.92 us -> none  [the longest x1 3.52 us: local(): devs = lax.psum(jnp.sum(centred_here * centred_here, axis=0), 'dp')]
    convert_element_type x1 -> x8, other arithmetic: 5.36 us -> 1.26 us  [the longest x6 0.91 us: normalize(): return ((x - mean) * scale + beta).astype(jnp.bfloat16)]
  transfers between devices with their start and end apart: 1 -> 22, of which waited for: 1 -> 9; matrix products, arithmetic and copies ran while one was open for 0% -> 1% of each run, Pallas kernels for 0% -> 13%
where the time goes in v1:
time: 101 us
  waiting for transfers between devices  62.7 us (62%)
  starting transfers between devices  18.5 us (18%)
  Pallas kernels  15.4 us (15%)
  local copies, waits for them, and re-layouts  2.83 us (3%)
  other arithmetic  1.34 us (1%)
    ppermute x7, waiting for transfers between devices, to_far(): lax.ppermute(x, 'feat', [(i, (i + s) % feat) for i in range(feat)])  56.9 us
    pallas_call x6, Pallas kernels, layer(): pl.pallas_call(functools.partial(layer_kernel, shards=shards), grid=(coun...  13.9 us
    ppermute x3, starting transfers between devices, local(): theirs = lax.ppermute(mine, 'dp', [(i, i ^ step) for i in range(dp)])  8.3 us
    ppermute x7, starting transfers between devices, to_far(): lax.ppermute(x, 'feat', [(i, (i + s) % feat) for i in range(feat)])  7.73 us
    ppermute x3, waiting for transfers between devices, local(): theirs = lax.ppermute(mine, 'dp', [(i, i ^ step) for i in range(dp)])  3.18 us
    unnamed x14, local copies, waits for them, and re-layouts  2.82 us
    ppermute x12, waiting for transfers between devices, to_near(): return lax.ppermute(x, 'feat', near)  2.61 us
    ppermute x12, starting transfers between devices, to_near(): return lax.ppermute(x, 'feat', near)  2.46 us
  transfers between devices with their start and end apart: 22, of which 9 were waited for; matrix products, arithmetic and copies ran while one was open for 1% of the time, Pallas kernels for 13%

profile of v1, /device:TPU:0, one launch (start us, length us, event | category | flops | bytes accessed | tf_op | source)
XLA Modules:
  0.0 101.0 jit_solution(7851802717560723222)
XLA Ops:
  0.0 2.8 %copy-done = f32[3072,512]{1,0:T(8,128)S(1)} copy-done((f32[3072,512]{1,0:T(8,128)S(1)}, f32[3072,512]{1,0:T(8,128)}, u32[]{:S(2)}) %copy-start) | copy-done | bytes 6291480
  2.8 0.5 shard_map.56
  3.5 0.8 shard_map.57
  4.4 3.0 %collective-permute-start = (f32[2,512]{1,0:T(2,128)S(1)}, f32[2,512]{1,0:T(2,128)S(1)}, u32[]{:S(2)}, u32[]{:S(2)}) collective-permute-start(f32[2,512]{1,0:T(2,128)S(1)} %shard_map.57), channel_id=1, source_target_pairs={{0,4},{4,0},{8,12},{12,8},{16,20},{20,16},{24,28},{28,24},{1,5},{5... | collective-permute-start | bytes 12296 | tf_op jit(solution)/shard_map/ppermute | solution.py:180
  7.4 1.6 %collective-permute-done = f32[2,512]{1,0:T(2,128)S(1)} collective-permute-done((f32[2,512]{1,0:T(2,128)S(1)}, f32[2,512]{1,0:T(2,128)S(1)}, u32[]{:S(2)}, u32[]{:S(2)}) %collective-permute-start) | collective-permute-done | bytes 4128 | tf_op jit(solution)/shard_map/ppermute | solution.py:180
  9.0 2.2 %collective-permute-start.1 = (f32[2,512]{1,0:T(2,128)S(1)}, f32[2,512]{1,0:T(2,128)S(1)}, u32[]{:S(2)}, u32[]{:S(2)}) collective-permute-start(f32[2,512]{1,0:T(2,128)S(1)} %pad_maximum_fusion.1), channel_id=1, source_target_pairs={{0,8},{4,12},{8,0},{12,4},{16,24},{20,28},{24,16},{28,20},{1,9},{5... | collective-permute-start | bytes 12296 | tf_op jit(solution)/shard_map/ppermute | solution.py:180
  11.2 1.6 %collective-permute-done.1 = f32[2,512]{1,0:T(2,128)S(1)} collective-permute-done((f32[2,512]{1,0:T(2,128)S(1)}, f32[2,512]{1,0:T(2,128)S(1)}, u32[]{:S(2)}, u32[]{:S(2)}) %collective-permute-start.1) | collective-permute-done | bytes 4128 | tf_op jit(solution)/shard_map/ppermute | solution.py:180
  12.8 3.1 %collective-permute-start.2 = (f32[2,512]{1,0:T(2,128)S(1)}, f32[2,512]{1,0:T(2,128)S(1)}, u32[]{:S(2)}, u32[]{:S(2)}) collective-permute-start(f32[2,512]{1,0:T(2,128)S(1)} %pad_maximum_fusion.2), channel_id=1, source_target_pairs={{0,16},{4,20},{8,24},{12,28},{16,0},{20,4},{24,8},{28,12},{1,17},{... | collective-permute-start | bytes 12296 | tf_op jit(solution)/shard_map/ppermute | solution.py:180
  15.9 1.5 %collective-permute-start.20 = (bf16[256,512]{1,0:T(8,128)(2,1)S(1)}, bf16[256,512]{1,0:T(8,128)(2,1)S(1)}, u32[]{:S(2)}, u32[]{:S(2)}) collective-permute-start(bf16[256,512]{1,0:T(8,128)(2,1)S(1)} %get-tuple-element.16), channel_id=1, source_target_pairs={{0,2},{1,3},{2,0},{3,1},{4,6},{5,7},{6,4},{7,5},{8,10},{9,11},{10,... | collective-permute-start | bytes 786440 | tf_op jit(solution)/shard_map/ppermute | solution.py:163
  17.4 0.5 collective-permute-start.16
  18.9 1.6 %collective-permute-start.17 = (f32[6,512]{1,0:T(8,128)S(1)}, f32[6,512]{1,0:T(8,128)S(1)}, u32[]{:S(2)}, u32[]{:S(2)}) collective-permute-start(f32[6,512]{1,0:T(8,128)S(1)} %pad_maximum_fusion), channel_id=1, source_target_pairs={{0,2},{1,3},{2,0},{3,1},{4,6},{5,7},{6,4},{7,5},{8,10},{9,11},{10,... | collective-permute-start | bytes 36872 | tf_op jit(solution)/shard_map/ppermute | solution.py:163
  20.5 0.5 collective-permute-start.4
  21.2 26.7 %collective-permute-done.17 = f32[6,512]{1,0:T(8,128)S(1)} collective-permute-done((f32[6,512]{1,0:T(8,128)S(1)}, f32[6,512]{1,0:T(8,128)S(1)}, u32[]{:S(2)}, u32[]{:S(2)}) %collective-permute-start.17) | collective-permute-done | bytes 12320 | tf_op jit(solution)/shard_map/ppermute | solution.py:163
  47.9 1.5 %collective-permute-start.13 = (bf16[768,512]{1,0:T(8,128)(2,1)S(1)}, bf16[768,512]{1,0:T(8,128)(2,1)S(1)}, u32[]{:S(2)}, u32[]{:S(2)}) collective-permute-start(bf16[768,512]{1,0:T(8,128)(2,1)S(1)} %add_convert_fusion.1.refs_0_), channel_id=1, source_target_pairs={{0,2},{1,3},{2,0},{3,1},{4,6},{5,7},{6,4},{7,5},{8,10},{9,11},{10,... | collective-permute-start | bytes 2359304 | tf_op jit(solution)/shard_map/ppermute | solution.py:163
  49.4 1.3 %collective-permute-done.4.refs_2_ = bf16[128,512]{1,0:T(8,128)(2,1)S(1)} collective-permute-done((bf16[128,512]{1,0:T(8,128)(2,1)S(1)}, bf16[128,512]{1,0:T(8,128)(2,1)S(1)}, u32[]{:S(2)}, u32[]{:S(2)}) %collective-permute-start.4) | collective-permute-done | bytes 131104 | tf_op jit(solution)/shard_map/ppermute | solution.py:163
  50.7 1.5 %collective-permute-start.7 = (bf16[384,512]{1,0:T(8,128)(2,1)S(1)}, bf16[384,512]{1,0:T(8,128)(2,1)S(1)}, u32[]{:S(2)}, u32[]{:S(2)}) collective-permute-start(bf16[384,512]{1,0:T(8,128)(2,1)S(1)} %add_convert_fusion.3.refs_0_), channel_id=1, source_target_pairs={{0,2},{1,3},{2,0},{3,1},{4,6},{5,7},{6,4},{7,5},{8,10},{9,11},{10,... | collective-permute-start | bytes 1179656 | tf_op jit(solution)/shard_map/ppermute | solution.py:163
  52.2 0.6 collective-permute-start.10
  53.0 23.8 %collective-permute-done.7.refs_2_ = bf16[384,512]{1,0:T(8,128)(2,1)S(1)} collective-permute-done((bf16[384,512]{1,0:T(8,128)(2,1)S(1)}, bf16[384,512]{1,0:T(8,128)(2,1)S(1)}, u32[]{:S(2)}, u32[]{:S(2)}) %collective-permute-start.7) | collective-permute-done | bytes 393248 | tf_op jit(solution)/shard_map/ppermute | solution.py:163
  76.7 0.5 collective-permute-start.12
  77.5 0.7 collective-permute-done.21.refs_3_
  78.4 5.1 %collective-permute-done.10.refs_2_ = bf16[512,512]{1,0:T(8,128)(2,1)S(1)} collective-permute-done((bf16[512,512]{1,0:T(8,128)(2,1)S(1)}, bf16[512,512]{1,0:T(8,128)(2,1)S(1)}, u32[]{:S(2)}, u32[]{:S(2)}) %collective-permute-start.10) | collective-permute-done | bytes 524320 | tf_op jit(solution)/shard_map/ppermute | solution.py:163
  83.5 0.5 collective-permute-start.14
  84.0 1.4 %collective-permute-done.9.refs_1_ = bf16[512,512]{1,0:T(8,128)(2,1)S(1)} collective-permute-done((bf16[512,512]{1,0:T(8,128)(2,1)S(1)}, bf16[512,512]{1,0:T(8,128)(2,1)S(1)}, u32[]{:S(2)}, u32[]{:S(2)}) %collective-permute-start.9) | collective-permute-done | bytes 524320 | tf_op jit(solution)/shard_map/ppermute | solution.py:166
  85.6 0.4 collective-permute-start.6
  86.1 0.5 collective-permute-done.14.refs_3_
  86.7 0.4 collective-permute-start.5
  87.1 1.5 %shard_map.58.refs_6_ = f32[3072,512]{1,0:T(8,128)} custom-call(bf16[256,512]{1,0:T(8,128)(2,1)S(1)} %add_convert_fusion.5.refs_0_, bf16[256,512]{1,0:T(8,128)(2,1)S(1)} %collective-permute-done.19.refs_1_, bf16[256,512]{1,0:T(8,128)(2,1)S(1)} %add_convert_fusion.4.refs_2_, bf16[256,512]{1,0:T(8,128)(2,1)S(1)} %collective-permute-done.21.refs_3_, ...), custom_call_target="tpu_custom_call" | custom-call | tf_op jit(solution)/shard_map/pallas_call | solution.py:142
  88.6 3.7 %shard_map.59.refs_6_ = f32[3072,512]{1,0:T(8,128)} custom-call(bf16[1024,512]{1,0:T(8,128)(2,1)S(1)} %add_convert_fusion.refs_0_, bf16[1024,512]{1,0:T(8,128)(2,1)S(1)} %collective-permute-done.15.refs_1_, bf16[1024,512]{1,0:T(8,128)(2,1)S(1)} %fusion.refs_2_, ...), custom_call_target="tpu_custom_call", output_to_operand_aliasing={{}: (6, {})} | custom-call | tf_op jit(solution)/shard_map/pallas_call | solution.py:142
  92.3 3.0 %shard_map.60.refs_6_ = f32[3072,512]{1,0:T(8,128)} custom-call(bf16[768,512]{1,0:T(8,128)(2,1)S(1)} %add_convert_fusion.1.refs_0_, bf16[768,512]{1,0:T(8,128)(2,1)S(1)} %collective-permute-done.12.refs_1_, bf16[768,512]{1,0:T(8,128)(2,1)S(1)} %collective-permute-done.13.refs_2_, ...), custom_call_target="tpu_custom_call", output_to_operand_aliasing={{}: (6, {})} | custom-call | tf_op jit(solution)/shard_map/pallas_call | solution.py:142
  95.3 2.2 %shard_map.61.refs_6_ = f32[3072,512]{1,0:T(8,128)} custom-call(bf16[512,512]{1,0:T(8,128)(2,1)S(1)} %add_convert_fusion.2.refs_0_, bf16[512,512]{1,0:T(8,128)(2,1)S(1)} %collective-permute-done.9.refs_1_, bf16[512,512]{1,0:T(8,128)(2,1)S(1)} %collective-permute-done.10.refs_2_, ...), custom_call_target="tpu_custom_call", output_to_operand_aliasing={{}: (6, {})} | custom-call | tf_op jit(solution)/shard_map/pallas_call | solution.py:142
  97.5 2.3 %shard_map.62.refs_6_ = f32[3072,512]{1,0:T(8,128)} custom-call(bf16[384,512]{1,0:T(8,128)(2,1)S(1)} %add_convert_fusion.3.refs_0_, bf16[384,512]{1,0:T(8,128)(2,1)S(1)} %collective-permute-done.6.refs_1_, bf16[384,512]{1,0:T(8,128)(2,1)S(1)} %collective-permute-done.7.refs_2_, ...), custom_call_target="tpu_custom_call", output_to_operand_aliasing={{}: (6, {})} | custom-call | tf_op jit(solution)/shard_map/pallas_call | solution.py:142
  99.8 1.1 %shard_map.63 = f32[3072,512]{1,0:T(8,128)} custom-call(bf16[128,512]{1,0:T(8,128)(2,1)S(1)} %add_convert_fusion.6.refs_0_, bf16[128,512]{1,0:T(8,128)(2,1)S(1)} %collective-permute-done.3.refs_1_, bf16[128,512]{1,0:T(8,128)(2,1)S(1)} %collective-permute-done.4.refs_2_, ...), custom_call_target="tpu_custom_call", output_to_operand_aliasing={{}: (6, {})} | custom-call | tf_op jit(solution)/shard_map/pallas_call | solution.py:142
  (54 shorter events, 2.2 us)
Async XLA Ops:
  0.0 2.8 %copy-start = (f32[3072,512]{1,0:T(8,128)S(1)}, f32[3072,512]{1,0:T(8,128)}, u32[]{:S(2)}) copy-start(f32[3072,512]{1,0:T(8,128)} %x_ref.5) | copy-start | bytes 18874372
  2.8 15.2 %slice-start = ((s8[6291456]{0:T(1024)(128)(4,1)}), s8[4194304]{0:T(1024)(128)(4,1)S(1)}, s32[]{:S(2)}) async-start(s8[6291456]{0:T(1024)(128)(4,1)} %bitcast.10), calls=%async_computation | async-start | bytes 8388608
  3.3 14.7 %slice-start.1 = ((s8[6291456]{0:T(1024)(128)(4,1)}), s8[2097152]{0:T(1024)(128)(4,1)S(1)}, s32[]{:S(2)}) async-start(s8[6291456]{0:T(1024)(128)(4,1)} %bitcast.10), calls=%async_computation.1 | async-start | bytes 4194304
  3.5 14.5 %copy-start.4 = (f32[512]{0:T(512)S(1)}, f32[512]{0:T(512)}, u32[]{:S(2)}) copy-start(f32[512]{0:T(512)} %param.6) | copy-start | bytes 6148
  3.5 14.5 %copy-start.3 = (f32[512]{0:T(512)S(1)}, f32[512]{0:T(512)}, u32[]{:S(2)}) copy-start(f32[512]{0:T(512)} %param.7) | copy-start | bytes 6148
  4.4 4.6 %collective-permute-start = (f32[2,512]{1,0:T(2,128)S(1)}, f32[2,512]{1,0:T(2,128)S(1)}, u32[]{:S(2)}, u32[]{:S(2)}) collective-permute-start(f32[2,512]{1,0:T(2,128)S(1)} %shard_map.57), channel_id=1, source_target_pairs={{0,4},{4,0},{8,12},{12,8},{16,20},{20,16},{24,28},{28,24},{1,5},{5... | collective-permute-start | bytes 12296 | tf_op jit(solution)/shard_map/ppermute | solution.py:180
  9.0 3.8 %collective-permute-start.1 = (f32[2,512]{1,0:T(2,128)S(1)}, f32[2,512]{1,0:T(2,128)S(1)}, u32[]{:S(2)}, u32[]{:S(2)}) collective-permute-start(f32[2,512]{1,0:T(2,128)S(1)} %pad_maximum_fusion.1), channel_id=1, source_target_pairs={{0,8},{4,12},{8,0},{12,4},{16,24},{20,28},{24,16},{28,20},{1,9},{5... | collective-permute-start | bytes 12296 | tf_op jit(solution)/shard_map/ppermute | solution.py:180
  12.8 5.1 %collective-permute-start.2 = (f32[2,512]{1,0:T(2,128)S(1)}, f32[2,512]{1,0:T(2,128)S(1)}, u32[]{:S(2)}, u32[]{:S(2)}) collective-permute-start(f32[2,512]{1,0:T(2,128)S(1)} %pad_maximum_fusion.2), channel_id=1, source_target_pairs={{0,16},{4,20},{8,24},{12,28},{16,0},{20,4},{24,8},{28,12},{1,17},{... | collective-permute-start | bytes 12296 | tf_op jit(solution)/shard_map/ppermute | solution.py:180
  15.9 36.3 %collective-permute-start.20 = (bf16[256,512]{1,0:T(8,128)(2,1)S(1)}, bf16[256,512]{1,0:T(8,128)(2,1)S(1)}, u32[]{:S(2)}, u32[]{:S(2)}) collective-permute-start(bf16[256,512]{1,0:T(8,128)(2,1)S(1)} %get-tuple-element.16), channel_id=1, source_target_pairs={{0,2},{1,3},{2,0},{3,1},{4,6},{5,7},{6,4},{7,5},{8,10},{9,11},{10,... | collective-permute-start | bytes 786440 | tf_op jit(solution)/shard_map/ppermute | solution.py:163
  17.4 59.3 %collective-permute-start.16 = (bf16[1024,512]{1,0:T(8,128)(2,1)S(1)}, bf16[1024,512]{1,0:T(8,128)(2,1)S(1)}, u32[]{:S(2)}, u32[]{:S(2)}) collective-permute-start(bf16[1024,512]{1,0:T(8,128)(2,1)S(1)} %get-tuple-element.15), channel_id=1, source_target_pairs={{0,2},{1,3},{2,0},{3,1},{4,6},{5,7},{6,4},{7,5},{8,10},{9,11},{10,... | collective-permute-start | bytes 3145736 | tf_op jit(solution)/shard_map/ppermute | solution.py:163
  18.8 68.2 %copy-start.1 = (bf16[2048,512]{1,0:T(8,128)(2,1)S(1)}, bf16[2048,512]{1,0:T(8,128)(2,1)}, u32[]{:S(2)}) copy-start(bf16[2048,512]{1,0:T(8,128)(2,1)} %refs_4_.11) | copy-start | bytes 6291460
  18.8 68.2 %copy-start.2 = (f32[512]{0:T(512)S(1)}, f32[512]{0:T(512)}, u32[]{:S(2)}) copy-start(f32[512]{0:T(512)} %param.9) | copy-start | bytes 6148
  18.9 29.0 %collective-permute-start.17 = (f32[6,512]{1,0:T(8,128)S(1)}, f32[6,512]{1,0:T(8,128)S(1)}, u32[]{:S(2)}, u32[]{:S(2)}) collective-permute-start(f32[6,512]{1,0:T(8,128)S(1)} %pad_maximum_fusion), channel_id=1, source_target_pairs={{0,2},{1,3},{2,0},{3,1},{4,6},{5,7},{6,4},{7,5},{8,10},{9,11},{10,... | collective-permute-start | bytes 36872 | tf_op jit(solution)/shard_map/ppermute | solution.py:163
  20.5 30.2 %collective-permute-start.4 = (bf16[128,512]{1,0:T(8,128)(2,1)S(1)}, bf16[128,512]{1,0:T(8,128)(2,1)S(1)}, u32[]{:S(2)}, u32[]{:S(2)}) collective-permute-start(bf16[128,512]{1,0:T(8,128)(2,1)S(1)} %add_convert_fusion.6.refs_0_), channel_id=1, source_target_pairs={{0,2},{1,3},{2,0},{3,1},{4,6},{5,7},{6,4},{7,5},{8,10},{9,11},{10,... | collective-permute-start | bytes 393224 | tf_op jit(solution)/shard_map/ppermute | solution.py:163
  21.1 31.8 %collective-permute-start.19 = (bf16[256,512]{1,0:T(8,128)(2,1)S(1)}, bf16[256,512]{1,0:T(8,128)(2,1)S(1)}, u32[]{:S(2)}, u32[]{:S(2)}) collective-permute-start(bf16[256,512]{1,0:T(8,128)(2,1)S(1)} %add_convert_fusion.5.refs_0_), channel_id=1, source_target_pairs={{0,1},{1,0},{2,3},{3,2},{4,5},{5,4},{6,7},{7,6},{8,9},{9,8},{10,11... | collective-permute-start | bytes 786440 | tf_op jit(solution)/shard_map/ppermute | solution.py:166
  47.9 35.6 %collective-permute-start.13 = (bf16[768,512]{1,0:T(8,128)(2,1)S(1)}, bf16[768,512]{1,0:T(8,128)(2,1)S(1)}, u32[]{:S(2)}, u32[]{:S(2)}) collective-permute-start(bf16[768,512]{1,0:T(8,128)(2,1)S(1)} %add_convert_fusion.1.refs_0_), channel_id=1, source_target_pairs={{0,2},{1,3},{2,0},{3,1},{4,6},{5,7},{6,4},{7,5},{8,10},{9,11},{10,... | collective-permute-start | bytes 2359304 | tf_op jit(solution)/shard_map/ppermute | solution.py:163
  50.7 26.0 %collective-permute-start.7 = (bf16[384,512]{1,0:T(8,128)(2,1)S(1)}, bf16[384,512]{1,0:T(8,128)(2,1)S(1)}, u32[]{:S(2)}, u32[]{:S(2)}) collective-permute-start(bf16[384,512]{1,0:T(8,128)(2,1)S(1)} %add_convert_fusion.3.refs_0_), channel_id=1, source_target_pairs={{0,2},{1,3},{2,0},{3,1},{4,6},{5,7},{6,4},{7,5},{8,10},{9,11},{10,... | collective-permute-start | bytes 1179656 | tf_op jit(solution)/shard_map/ppermute | solution.py:163
  52.2 31.3 %collective-permute-start.10 = (bf16[512,512]{1,0:T(8,128)(2,1)S(1)}, bf16[512,512]{1,0:T(8,128)(2,1)S(1)}, u32[]{:S(2)}, u32[]{:S(2)}) collective-permute-start(bf16[512,512]{1,0:T(8,128)(2,1)S(1)} %add_convert_fusion.2.refs_0_), channel_id=1, source_target_pairs={{0,2},{1,3},{2,0},{3,1},{4,6},{5,7},{6,4},{7,5},{8,10},{9,11},{10,... | collective-permute-start | bytes 1572872 | tf_op jit(solution)/shard_map/ppermute | solution.py:163
  52.9 33.0 %collective-permute-start.15 = (bf16[1024,512]{1,0:T(8,128)(2,1)S(1)}, bf16[1024,512]{1,0:T(8,128)(2,1)S(1)}, u32[]{:S(2)}, u32[]{:S(2)}) collective-permute-start(bf16[1024,512]{1,0:T(8,128)(2,1)S(1)} %add_convert_fusion.refs_0_), channel_id=1, source_target_pairs={{0,1},{1,0},{2,3},{3,2},{4,5},{5,4},{6,7},{7,6},{8,9},{9,8},{10,11... | collective-permute-start | bytes 3145736 | tf_op jit(solution)/shard_map/ppermute | solution.py:166
  76.7 1.5 %collective-permute-start.21 = (bf16[256,512]{1,0:T(8,128)(2,1)S(1)}, bf16[256,512]{1,0:T(8,128)(2,1)S(1)}, u32[]{:S(2)}, u32[]{:S(2)}) collective-permute-start(bf16[256,512]{1,0:T(8,128)(2,1)S(1)} %add_convert_fusion.4.refs_2_), channel_id=1, source_target_pairs={{0,1},{1,0},{2,3},{3,2},{4,5},{5,4},{6,7},{7,6},{8,9},{9,8},{10,11... | collective-permute-start | bytes 786440 | tf_op jit(solution)/shard_map/ppermute | solution.py:166
  76.7 8.8 %collective-permute-start.12 = (bf16[768,512]{1,0:T(8,128)(2,1)S(1)}, bf16[768,512]{1,0:T(8,128)(2,1)S(1)}, u32[]{:S(2)}, u32[]{:S(2)}) collective-permute-start(bf16[768,512]{1,0:T(8,128)(2,1)S(1)} %add_convert_fusion.1.refs_0_), channel_id=1, source_target_pairs={{0,1},{1,0},{2,3},{3,2},{4,5},{5,4},{6,7},{7,6},{8,9},{9,8},{10,11... | collective-permute-start | bytes 2359304 | tf_op jit(solution)/shard_map/ppermute | solution.py:166
  78.3 8.4 %collective-permute-start.18 = (bf16[1024,512]{1,0:T(8,128)(2,1)S(1)}, bf16[1024,512]{1,0:T(8,128)(2,1)S(1)}, u32[]{:S(2)}, u32[]{:S(2)}) collective-permute-start(bf16[1024,512]{1,0:T(8,128)(2,1)S(1)} %fusion.refs_2_), channel_id=1, source_target_pairs={{0,1},{1,0},{2,3},{3,2},{4,5},{5,4},{6,7},{7,6},{8,9},{9,8},{10,11... | collective-permute-start | bytes 3145736 | tf_op jit(solution)/shard_map/ppermute | solution.py:166
  83.5 1.9 %collective-permute-start.9 = (bf16[512,512]{1,0:T(8,128)(2,1)S(1)}, bf16[512,512]{1,0:T(8,128)(2,1)S(1)}, u32[]{:S(2)}, u32[]{:S(2)}) collective-permute-start(bf16[512,512]{1,0:T(8,128)(2,1)S(1)} %add_convert_fusion.2.refs_0_), channel_id=1, source_target_pairs={{0,1},{1,0},{2,3},{3,2},{4,5},{5,4},{6,7},{7,6},{8,9},{9,8},{10,11... | collective-permute-start | bytes 1572872 | tf_op jit(solution)/shard_map/ppermute | solution.py:166
  83.5 3.0 %collective-permute-start.14 = (bf16[768,512]{1,0:T(8,128)(2,1)S(1)}, bf16[768,512]{1,0:T(8,128)(2,1)S(1)}, u32[]{:S(2)}, u32[]{:S(2)}) collective-permute-start(bf16[768,512]{1,0:T(8,128)(2,1)S(1)} %collective-permute-done.13.refs_2_), channel_id=1, source_target_pairs={{0,1},{1,0},{2,3},{3,2},{4,5},{5,4},{6,7},{7,6},{8,9},{9,8},{10,11... | collective-permute-start | bytes 2359304 | tf_op jit(solution)/shard_map/ppermute | solution.py:166
  85.4 9.9 %collective-permute-start.11 = (bf16[512,512]{1,0:T(8,128)(2,1)S(1)}, bf16[512,512]{1,0:T(8,128)(2,1)S(1)}, u32[]{:S(2)}, u32[]{:S(2)}) collective-permute-start(bf16[512,512]{1,0:T(8,128)(2,1)S(1)} %collective-permute-done.10.refs_2_), channel_id=1, source_target_pairs={{0,1},{1,0},{2,3},{3,2},{4,5},{5,4},{6,7},{7,6},{8,9},{9,8},{10,11... | collective-permute-start | bytes 1572872 | tf_op jit(solution)/shard_map/ppermute | solution.py:166
  85.6 12.0 %collective-permute-start.6 = (bf16[384,512]{1,0:T(8,128)(2,1)S(1)}, bf16[384,512]{1,0:T(8,128)(2,1)S(1)}, u32[]{:S(2)}, u32[]{:S(2)}) collective-permute-start(bf16[384,512]{1,0:T(8,128)(2,1)S(1)} %add_convert_fusion.3.refs_0_), channel_id=1, source_target_pairs={{0,1},{1,0},{2,3},{3,2},{4,5},{5,4},{6,7},{7,6},{8,9},{9,8},{10,11... | collective-permute-start | bytes 1179656 | tf_op jit(solution)/shard_map/ppermute | solution.py:166
  85.9 11.6 %collective-permute-start.8 = (bf16[384,512]{1,0:T(8,128)(2,1)S(1)}, bf16[384,512]{1,0:T(8,128)(2,1)S(1)}, u32[]{:S(2)}, u32[]{:S(2)}) collective-permute-start(bf16[384,512]{1,0:T(8,128)(2,1)S(1)} %collective-permute-done.7.refs_2_), channel_id=1, source_target_pairs={{0,1},{1,0},{2,3},{3,2},{4,5},{5,4},{6,7},{7,6},{8,9},{9,8},{10,11... | collective-permute-start | bytes 1179656 | tf_op jit(solution)/shard_map/ppermute | solution.py:166
  86.5 13.3 %collective-permute-start.3 = (bf16[128,512]{1,0:T(8,128)(2,1)S(1)}, bf16[128,512]{1,0:T(8,128)(2,1)S(1)}, u32[]{:S(2)}, u32[]{:S(2)}) collective-permute-start(bf16[128,512]{1,0:T(8,128)(2,1)S(1)} %add_convert_fusion.6.refs_0_), channel_id=1, source_target_pairs={{0,1},{1,0},{2,3},{3,2},{4,5},{5,4},{6,7},{7,6},{8,9},{9,8},{10,11... | collective-permute-start | bytes 393224 | tf_op jit(solution)/shard_map/ppermute | solution.py:166
  86.7 13.1 %collective-permute-start.5 = (bf16[128,512]{1,0:T(8,128)(2,1)S(1)}, bf16[128,512]{1,0:T(8,128)(2,1)S(1)}, u32[]{:S(2)}, u32[]{:S(2)}) collective-permute-start(bf16[128,512]{1,0:T(8,128)(2,1)S(1)} %collective-permute-done.4.refs_2_), channel_id=1, source_target_pairs={{0,1},{1,0},{2,3},{3,2},{4,5},{5,4},{6,7},{7,6},{8,9},{9,8},{10,11... | collective-permute-start | bytes 393224 | tf_op jit(solution)/shard_map/ppermute | solution.py:166

commit v2 on v0

v2 whole, which is shorter than its diff:
```python
import functools

import jax
import jax.numpy as jnp
from jax import lax
from jax.experimental import pallas as pl
from jax.experimental.pallas import tpu as pltpu
from jax.sharding import PartitionSpec as P


UNITS = 24
EARLY = (2, 6)
LATE = (7, 4, 3, 1, 1)
PIECE = 2
SPLIT = 3


def grant(kib):
    return pltpu.CompilerParams(vmem_limit_bytes=kib * 1024)


def centred(x):
    mean = jnp.mean(x, axis=0, keepdims=True)
    d = x - mean
    return d.astype(jnp.bfloat16), mean, jnp.sum(d * d, axis=0, keepdims=True)


def centre_kernel(x_ref, sent_ref, stat_ref, buf, sem):
    copy = pltpu.make_async_copy(x_ref.at[pl.ds(0, buf.shape[0]), :], buf, sem)
    copy.start()
    copy.wait()
    sent, mean, dev = centred(buf[...])
    sent_ref[...] = sent
    stat_ref[0:1, :] = mean
    stat_ref[1:2, :] = dev


def centre(features, count):
    cols = features.shape[1]
    return pl.pallas_call(
        centre_kernel,
        in_specs=[pl.BlockSpec(memory_space=pltpu.HBM)],
        out_specs=[pl.BlockSpec(memory_space=pltpu.VMEM)] * 2,
        out_shape=[
            jax.ShapeDtypeStruct((count, cols), jnp.bfloat16),
            jax.ShapeDtypeStruct((2, cols), jnp.float32),
        ],
        scratch_shapes=[pltpu.VMEM((count, cols), jnp.float32), pltpu.SemaphoreType.DMA],
        compiler_params=grant(51000),
    )(features)


def survey_kernel(x_ref, stat_ref, held_ref, sent_ref, means_ref, total_ref, sems, *, first, early, piece):
    rows, cols = held_ref.shape
    pieces = rows // piece
    order = [p for p in range(pieces) if p * piece >= first] + [p for p in range(pieces) if p * piece < first]
    copies = {}
    for p in order:
        place = pl.ds(p * piece, piece)
        copies[p] = pltpu.make_async_copy(x_ref.at[place, :], held_ref.at[place, :], sems.at[p])
        copies[p].start()
    pivot = stat_ref[0:1, :]
    groups = [(first, pivot, stat_ref[1:2, :])]
    sums = jnp.zeros((8, cols), jnp.float32)
    devs = jnp.zeros((8, cols), jnp.float32)
    rest = 0
    for p in order:
        copies[p].wait()
        if p * piece < first:
            continue
        x = held_ref[pl.ds(p * piece, piece), :]
        if p * piece < first + early:
            sent, mean, dev = centred(x)
            sent_ref[pl.ds(p * piece - first, piece), :] = sent
            means_ref[pl.ds(p - first // piece, 1), :] = mean
            groups.append((piece, mean, dev))
        else:
            d = (x - pivot).reshape(-1, 8, cols)
            sums = sums + jnp.sum(d, axis=0)
            devs = devs + jnp.sum(d * d, axis=0)
            rest += piece
    shift = jnp.sum(sums, axis=0, keepdims=True) / rest
    dev = jnp.sum(devs, axis=0, keepdims=True) - rest * (shift * shift)
    groups.append((rest, pivot + shift, dev))
    mean = sum(n * m for n, m, _ in groups) / rows
    dev = sum(d + n * ((m - mean) * (m - mean)) for n, m, d in groups)
    total_ref[0:1, :] = mean
    total_ref[1:2, :] = dev


def survey(features, stat, first, early, piece):
    rows, cols = features.shape
    return pl.pallas_call(
        functools.partial(survey_kernel, first=first, early=early, piece=piece),
        in_specs=[pl.BlockSpec(memory_space=pltpu.HBM), pl.BlockSpec(memory_space=pltpu.VMEM)],
        out_specs=[pl.BlockSpec(memory_space=pltpu.VMEM)] * 4,
        out_shape=[
            jax.ShapeDtypeStruct((rows, cols), jnp.float32),
            jax.ShapeDtypeStruct((early, cols), jnp.bfloat16),
            jax.ShapeDtypeStruct((early // piece, cols), jnp.float32),
            jax.ShapeDtypeStruct((2, cols), jnp.float32),
        ],
        scratch_shapes=[pltpu.SemaphoreType.DMA((rows // piece,))],
        compiler_params=grant(46000),
    )(features, stat)


def shard_order():
    feat = lax.axis_size("feat")
    me = lax.axis_index("feat")
    order = [me, me ^ 1]
    for s in range(2, feat, 2):
        source = (me - s) % feat
        order += [source, source ^ 1]
    return order


def product(xs, places, w_ref, total, rows):
    cols = xs[0].shape[1]
    order = shard_order()
    for x, place in zip(xs, places):
        start = pl.multiple_of(order[place] * cols, cols)
        w = w_ref[pl.ds(start, cols), :]
        total = total + jnp.dot(x[rows, :], w, preferred_element_type=jnp.float32)
    return total


def part_kernel(*refs, places):
    n = len(places)
    xs, (w_ref, bias_ref, out_ref) = refs[:n], refs[n:]
    out_ref[...] = product(xs, places, w_ref, bias_ref[...], pl.ds(0, xs[0].shape[0]))


def part(xs, places, weight, bias):
    return pl.pallas_call(
        functools.partial(part_kernel, places=places),
        in_specs=[pl.BlockSpec(memory_space=pltpu.VMEM)] * (len(xs) + 2),
        out_specs=pl.BlockSpec(memory_space=pltpu.VMEM),
        out_shape=jax.ShapeDtypeStruct((xs[0].shape[0], weight.shape[1]), jnp.float32),
        compiler_params=grant(12288),
    )(*xs, weight, bias)


def layer_kernel(*refs, places, first, block):
    n = len(places)
    xs, (w_ref, base_ref) = refs[:n], refs[n : n + 2]
    out_ref, buf, sems = refs[-3:]
    copies = []
    for b in range(xs[0].shape[0] // block):
        rows = pl.ds(b * block, block)
        base = base_ref[...] if base_ref.shape[0] == 1 else base_ref[rows, :]
        buf[rows, :] = jnp.maximum(product(xs, places, w_ref, base, rows), 0.0)
        copies.append(
            pltpu.make_async_copy(buf.at[rows, :], out_ref.at[pl.ds(first + b * block, block), :], sems.at[b])
        )
        copies[-1].start()
    for copy in copies:
        copy.wait()


def layer(xs, places, weight, base, out, first, rows, unit):
    count = xs[0].shape[0]
    width = weight.shape[1]
    block = 2 * unit if count % (2 * unit) == 0 else unit
    in_specs = [pl.BlockSpec(memory_space=pltpu.VMEM)] * (len(xs) + 2)
    args = [*xs, weight, base]
    aliases = {}
    if out is not None:
        in_specs += [pl.BlockSpec(memory_space=pltpu.HBM)]
        aliases = {len(args): 0}
        args += [out]
    return pl.pallas_call(
        functools.partial(layer_kernel, places=places, first=first, block=block),
        in_specs=in_specs,
        out_specs=pl.BlockSpec(memory_space=pltpu.HBM),
        out_shape=jax.ShapeDtypeStruct((rows, width), jnp.float32),
        input_output_aliases=aliases,
        scratch_shapes=[pltpu.VMEM((count, width), jnp.float32), pltpu.SemaphoreType.DMA((count // block,))],
        compiler_params=grant(12288),
    )(*args)


def local(features, gamma, beta, weight, bias):
    rows, cols = features.shape
    dp = lax.axis_size("dp")
    feat = lax.axis_size("feat")
    unit = rows // UNITS
    total_rows = rows * dp
    near = [(i, i ^ 1) for i in range(feat)]
    shifts = range(2, feat, 2)

    def to_far(x):
        return [lax.ppermute(x, "feat", [(i, (i + s) % feat) for i in range(feat)]) for s in shifts]

    def to_near(x):
        return lax.ppermute(x, "feat", near)

    firsts = [0]
    for count in EARLY + LATE:
        firsts.append(firsts[-1] + count)
    piece = PIECE * unit
    sizes = [EARLY[0] * unit, piece]
    sent, stat = centre(features, EARLY[0] * unit)
    early = [to_far(sent)]
    features, sent, means, mine = survey(features, stat, EARLY[0] * unit, EARLY[1] * unit, piece)
    early.append(to_far(sent))
    found = [stat[:1], means]
    step, held = 1, rows
    while step < dp:
        theirs = lax.ppermute(mine, "dp", [(i, i ^ step) for i in range(dp)])
        gap = mine[0] - theirs[0]
        mean = (mine[0] + theirs[0]) * 0.5
        dev = mine[1] + theirs[1] + (0.5 * held) * (gap * gap)
        mine = jnp.stack([mean, dev])
        step, held = 2 * step, 2 * held
    mean = mine[0]
    var = mine[1] / total_rows
    scale = gamma / jnp.sqrt(var + 1e-05)

    def normalize(k):
        x = features[firsts[k] * unit : firsts[k + 1] * unit]
        return ((x - mean) * scale + beta).astype(jnp.bfloat16)

    own, arrived = {}, {}
    for k in range(len(EARLY), len(EARLY) + len(LATE)):
        own[k] = normalize(k)
        arrived[k] = to_far(own[k])
    offsets = (jnp.concatenate(found) - mean) * scale + beta
    table = to_far(jnp.concatenate([scale[None], offsets]))
    row = 1
    for k, means in enumerate(found):
        own[k] = normalize(k)
        arrived[k] = []
        blocks = means.shape[0]
        for got, t in zip(early[k], table):
            got = got.reshape(blocks, sizes[k], cols).astype(jnp.float32)
            got = got * t[0] + t[row : row + blocks][:, None, :]
            arrived[k].append(got.astype(jnp.bfloat16).reshape(blocks * sizes[k], cols))
        row += blocks

    out = None
    bias = bias[None]
    for k in range(len(EARLY) + len(LATE)):
        xs = [own[k], to_near(own[k])]
        for got in arrived[k]:
            xs += [got, to_near(got)]
        places = tuple(range(len(xs)))
        base = bias
        if k >= len(EARLY) + len(LATE) - SPLIT:
            passed = places[3::2]
            held = tuple(p for p in places if p not in passed)
            base = part([xs[p] for p in held], held, weight, bias)
            places, xs = passed, [xs[p] for p in passed]
        out = layer(xs, places, weight, base, out, firsts[k] * unit, rows, unit)
    return out


def solution(mesh):
    placed = (P("dp", "feat"), P("feat"), P("feat"), P(None, "feat"), P("feat"))
    return jax.shard_map(local, mesh=mesh, in_specs=placed, out_specs=P("dp", "feat"), check_vma=False)
```

time: 159 us -> 105 us (0.66)
  blocking collectives: 40.2 us -> 0 us
  starting transfers between devices: 0.01 us -> 21.1 us
  Pallas kernels: 0 us -> 17.8 us
  waiting for transfers between devices: 81 us -> 64.3 us
  between operations: 13.4 us -> 0.29 us
  matrix products: 11.3 us -> 0 us
  other arithmetic: 12.3 us -> 1.24 us
    all_gather x1 -> x0, waiting for transfers between devices: 81 us -> none  [local(): lax.all_gather(normed, 'feat', axis=1, tiled=True)]
    ppermute x0 -> x25, waiting for transfers between devices: none -> 64.3 us  [the longest x8 59.9 us: to_far(): lax.ppermute(x, 'feat', [(i, (i + s) % feat) for i in range(feat)])]
    psum x2 -> x0, blocking collectives: 40.2 us -> none  [the longest x1 23.1 us: local(): sums = lax.psum(jnp.sum(features, axis=0), 'dp')]
    ppermute x0 -> x25, starting transfers between devices: none -> 21.1 us  [the longest x8 10.3 us: to_far(): lax.ppermute(x, 'feat', [(i, (i + s) % feat) for i in range(feat)])]
    pallas_call x0 -> x12, Pallas kernels: none -> 17.8 us  [the longest x7 12.2 us: layer(): pl.pallas_call(functools.partial(layer_kernel, places=places, first=first...]
    dot_general x1 -> x0, matrix products: 11.3 us -> none  [local(): jnp.dot(lax.all_gather(normed, 'feat', axis=1, tiled=True), weight, prefe...]
    reduce_sum x2 -> x0, other arithmetic: 6.92 us -> none  [the longest x1 3.52 us: local(): devs = lax.psum(jnp.sum(centred_here * centred_here, axis=0), 'dp')]
    convert_element_type x1 -> x8, other arithmetic: 5.36 us -> 1.16 us  [the longest x6 0.89 us: normalize(): return ((x - mean) * scale + beta).astype(jnp.bfloat16)]
  transfers between devices with their start and end apart: 1 -> 25, of which waited for: 1 -> 7; matrix products, arithmetic and copies ran while one was open for 0% -> 1% of each run, Pallas kernels for 0% -> 12%
where the time goes in v2:
time: 105 us
  waiting for transfers between devices  64.3 us (61%)
  starting transfers between devices  21.1 us (20%)
  Pallas kernels  17.8 us (17%)
  other arithmetic  1.24 us (1%)
    ppermute x8, waiting for transfers between devices, to_far(): lax.ppermute(x, 'feat', [(i, (i + s) % feat) for i in range(feat)])  59.9 us
    pallas_call x7, Pallas kernels, layer(): pl.pallas_call(functools.partial(layer_kernel, places=places, first=first...  12.2 us
    ppermute x8, starting transfers between devices, to_far(): lax.ppermute(x, 'feat', [(i, (i + s) % feat) for i in range(feat)])  10.3 us
    ppermute x3, starting transfers between devices, local(): theirs = lax.ppermute(mine, 'dp', [(i, i ^ step) for i in range(dp)])  8.3 us
    ppermute x3, waiting for transfers between devices, local(): theirs = lax.ppermute(mine, 'dp', [(i, i ^ step) for i in range(dp)])  3.18 us
    pallas_call x1, Pallas kernels, survey(): pl.pallas_call(functools.partial(survey_kernel, first=first, early=early,...  2.93 us
    ppermute x14, starting transfers between devices, to_near(): return lax.ppermute(x, 'feat', near)  2.42 us
  transfers between devices with their start and end apart: 25, of which 7 were waited for; matrix products, arithmetic and copies ran while one was open for 1% of the time, Pallas kernels for 12%

profile of v2, /device:TPU:0, one launch (start us, length us, event | category | flops | bytes accessed | tf_op | source)
XLA Modules:
  0.0 104.7 jit_solution(1745041723329224722)
XLA Ops:
  0.0 1.2 %shard_map.55 = (bf16[256,512]{1,0:T(8,128)(2,1)S(1)}, f32[2,512]{1,0:T(2,128)S(1)}) custom-call(f32[3072,512]{1,0:T(8,128)} %x_ref.3), custom_call_target="tpu_custom_call" | custom-call | tf_op jit(solution)/shard_map/pallas_call | solution.py:40
  1.2 2.9 %shard_map.56 = (f32[3072,512]{1,0:T(8,128)S(1)}, bf16[768,512]{1,0:T(8,128)(2,1)S(1)}, f32[3,512]{1,0:T(4,128)S(1)}, f32[2,512]{1,0:T(2,128)S(1)}) custom-call(f32[3072,512]{1,0:T(8,128)} %x_ref.3, f32[2,512]{1,0:T(2,128)S(1)} %get-tuple-element.11.stat_ref), custom_call_target="tpu_custom_call" | custom-call | tf_op jit(solution)/shard_map/pallas_call | solution.py:93
  4.1 3.0 %collective-permute-start = (f32[2,512]{1,0:T(2,128)S(1)}, f32[2,512]{1,0:T(2,128)S(1)}, u32[]{:S(2)}, u32[]{:S(2)}) collective-permute-start(f32[2,512]{1,0:T(2,128)S(1)} %get-tuple-element.13), channel_id=1, source_target_pairs={{0,4},{4,0},{8,12},{12,8},{16,20},{20,16},{24,28},{28,24},{1,5},{5... | collective-permute-start | bytes 12296 | tf_op jit(solution)/shard_map/ppermute | solution.py:210
  7.2 1.6 %collective-permute-done = f32[2,512]{1,0:T(2,128)S(1)} collective-permute-done((f32[2,512]{1,0:T(2,128)S(1)}, f32[2,512]{1,0:T(2,128)S(1)}, u32[]{:S(2)}, u32[]{:S(2)}) %collective-permute-start) | collective-permute-done | bytes 4128 | tf_op jit(solution)/shard_map/ppermute | solution.py:210
  8.8 2.2 %collective-permute-start.1 = (f32[2,512]{1,0:T(2,128)S(1)}, f32[2,512]{1,0:T(2,128)S(1)}, u32[]{:S(2)}, u32[]{:S(2)}) collective-permute-start(f32[2,512]{1,0:T(2,128)S(1)} %pad_maximum_fusion.1), channel_id=1, source_target_pairs={{0,8},{4,12},{8,0},{12,4},{16,24},{20,28},{24,16},{28,20},{1,9},{5... | collective-permute-start | bytes 12296 | tf_op jit(solution)/shard_map/ppermute | solution.py:210
  11.0 1.6 %collective-permute-done.1 = f32[2,512]{1,0:T(2,128)S(1)} collective-permute-done((f32[2,512]{1,0:T(2,128)S(1)}, f32[2,512]{1,0:T(2,128)S(1)}, u32[]{:S(2)}, u32[]{:S(2)}) %collective-permute-start.1) | collective-permute-done | bytes 4128 | tf_op jit(solution)/shard_map/ppermute | solution.py:210
  12.6 3.1 %collective-permute-start.2 = (f32[2,512]{1,0:T(2,128)S(1)}, f32[2,512]{1,0:T(2,128)S(1)}, u32[]{:S(2)}, u32[]{:S(2)}) collective-permute-start(f32[2,512]{1,0:T(2,128)S(1)} %pad_maximum_fusion.2), channel_id=1, source_target_pairs={{0,16},{4,20},{8,24},{12,28},{16,0},{20,4},{24,8},{28,12},{1,17},{... | collective-permute-start | bytes 12296 | tf_op jit(solution)/shard_map/ppermute | solution.py:210
  15.7 1.5 %collective-permute-start.23 = (bf16[256,512]{1,0:T(8,128)(2,1)S(1)}, bf16[256,512]{1,0:T(8,128)(2,1)S(1)}, u32[]{:S(2)}, u32[]{:S(2)}) collective-permute-start(bf16[256,512]{1,0:T(8,128)(2,1)S(1)} %get-tuple-element.16), channel_id=1, source_target_pairs={{0,2},{1,3},{2,0},{3,1},{4,6},{5,7},{6,4},{7,5},{8,10},{9,11},{10,... | collective-permute-start | bytes 786440 | tf_op jit(solution)/shard_map/ppermute | solution.py:193
  17.2 0.5 collective-permute-start.19
  18.3 1.6 %collective-permute-start.6 = (bf16[128,512]{1,0:T(8,128)(2,1)S(1)}, bf16[128,512]{1,0:T(8,128)(2,1)S(1)}, u32[]{:S(2)}, u32[]{:S(2)}) collective-permute-start(bf16[128,512]{1,0:T(8,128)(2,1)S(1)} %get-tuple-element.17.refs_0_), channel_id=1, source_target_pairs={{0,2},{1,3},{2,0},{3,1},{4,6},{5,7},{6,4},{7,5},{8,10},{9,11},{10,... | collective-permute-start | bytes 393224 | tf_op jit(solution)/shard_map/ppermute | solution.py:193
  20.0 0.6 collective-permute-start.20
  20.6 21.5 %collective-permute-done.20 = f32[5,512]{1,0:T(8,128)S(1)} collective-permute-done((f32[5,512]{1,0:T(8,128)S(1)}, f32[5,512]{1,0:T(8,128)S(1)}, u32[]{:S(2)}, u32[]{:S(2)}) %collective-permute-start.20) | collective-permute-done | bytes 10272 | tf_op jit(solution)/shard_map/ppermute | solution.py:193
  42.2 1.5 %collective-permute-start.3 = (bf16[128,512]{1,0:T(8,128)(2,1)S(1)}, bf16[128,512]{1,0:T(8,128)(2,1)S(1)}, u32[]{:S(2)}, u32[]{:S(2)}) collective-permute-start(bf16[128,512]{1,0:T(8,128)(2,1)S(1)} %get-tuple-element.18.refs_0_), channel_id=1, source_target_pairs={{0,2},{1,3},{2,0},{3,1},{4,6},{5,7},{6,4},{7,5},{8,10},{9,11},{10,... | collective-permute-start | bytes 393224 | tf_op jit(solution)/shard_map/ppermute | solution.py:193
  43.7 0.6 collective-permute-start.16
  44.3 3.2 %collective-permute-done.3.refs_2_ = bf16[128,512]{1,0:T(8,128)(2,1)S(1)} collective-permute-done((bf16[128,512]{1,0:T(8,128)(2,1)S(1)}, bf16[128,512]{1,0:T(8,128)(2,1)S(1)}, u32[]{:S(2)}, u32[]{:S(2)}) %collective-permute-start.3) | collective-permute-done | bytes 131104 | tf_op jit(solution)/shard_map/ppermute | solution.py:193
  47.5 2.5 %collective-permute-start.9 = (bf16[384,512]{1,0:T(8,128)(2,1)S(1)}, bf16[384,512]{1,0:T(8,128)(2,1)S(1)}, u32[]{:S(2)}, u32[]{:S(2)}) collective-permute-start(bf16[384,512]{1,0:T(8,128)(2,1)S(1)} %add_convert_fusion.3.refs_0_), channel_id=1, source_target_pairs={{0,2},{1,3},{2,0},{3,1},{4,6},{5,7},{6,4},{7,5},{8,10},{9,11},{10,... | collective-permute-start | bytes 1179656 | tf_op jit(solution)/shard_map/ppermute | solution.py:193
  50.3 1.2 %collective-permute-done.22.refs_1_ = bf16[256,512]{1,0:T(8,128)(2,1)S(1)} collective-permute-done((bf16[256,512]{1,0:T(8,128)(2,1)S(1)}, bf16[256,512]{1,0:T(8,128)(2,1)S(1)}, u32[]{:S(2)}, u32[]{:S(2)}) %collective-permute-start.22) | collective-permute-done | bytes 262176 | tf_op jit(solution)/shard_map/ppermute | solution.py:196
  52.1 23.2 %collective-permute-done.9.refs_2_ = bf16[384,512]{1,0:T(8,128)(2,1)S(1)} collective-permute-done((bf16[384,512]{1,0:T(8,128)(2,1)S(1)}, bf16[384,512]{1,0:T(8,128)(2,1)S(1)}, u32[]{:S(2)}, u32[]{:S(2)}) %collective-permute-start.9) | collective-permute-done | bytes 393248 | tf_op jit(solution)/shard_map/ppermute | solution.py:193
  75.4 1.6 %collective-permute-start.13 = (bf16[512,512]{1,0:T(8,128)(2,1)S(1)}, bf16[512,512]{1,0:T(8,128)(2,1)S(1)}, u32[]{:S(2)}, u32[]{:S(2)}) collective-permute-start(bf16[512,512]{1,0:T(8,128)(2,1)S(1)} %add_convert_fusion.2.refs_0_), channel_id=1, source_target_pairs={{0,2},{1,3},{2,0},{3,1},{4,6},{5,7},{6,4},{7,5},{8,10},{9,11},{10,... | collective-permute-start | bytes 1572872 | tf_op jit(solution)/shard_map/ppermute | solution.py:193
  77.8 12.0 %collective-permute-done.13.refs_2_ = bf16[512,512]{1,0:T(8,128)(2,1)S(1)} collective-permute-done((bf16[512,512]{1,0:T(8,128)(2,1)S(1)}, bf16[512,512]{1,0:T(8,128)(2,1)S(1)}, u32[]{:S(2)}, u32[]{:S(2)}) %collective-permute-start.13) | collective-permute-done | bytes 524320 | tf_op jit(solution)/shard_map/ppermute | solution.py:193
  89.8 0.5 collective-permute-start.14
  90.4 0.4 collective-permute-start.7
  90.9 0.4 shard_map.58.refs_2_
  91.3 0.4 shard_map.57.refs_2_
  91.7 0.8 shard_map.59.refs_2_
  92.5 1.5 %shard_map.60.refs_6_ = f32[3072,512]{1,0:T(8,128)} custom-call(bf16[256,512]{1,0:T(8,128)(2,1)S(1)} %add_convert_fusion.5.refs_0_, bf16[256,512]{1,0:T(8,128)(2,1)S(1)} %collective-permute-done.22.refs_1_, bf16[256,512]{1,0:T(8,128)(2,1)S(1)} %add_convert_fusion.4.refs_2_, bf16[256,512]{1,0:T(8,128)(2,1)S(1)} %collective-permute-done.24.refs_3_, ...), custom_call_target="tpu_custom_call" | custom-call | tf_op jit(solution)/shard_map/pallas_call | solution.py:172
  94.0 2.6 %shard_map.61.refs_6_ = f32[3072,512]{1,0:T(8,128)} custom-call(bf16[768,512]{1,0:T(8,128)(2,1)S(1)} %add_convert_fusion.1.refs_0_, bf16[768,512]{1,0:T(8,128)(2,1)S(1)} %collective-permute-done.18.refs_1_, bf16[768,512]{1,0:T(8,128)(2,1)S(1)} %fusion.refs_2_, bf16[768,512]{1,0:T(8,128)(2,1)S(1)} %collective-permute-done.21.refs_3_, ...), custom_call_target="tpu_custom_call", output_to_operand_aliasing={{}: (6, {})} | custom-call | tf_op jit(solution)/shard_map/pallas_call | solution.py:172
  96.6 2.8 %shard_map.62.refs_6_ = f32[3072,512]{1,0:T(8,128)} custom-call(bf16[896,512]{1,0:T(8,128)(2,1)S(1)} %add_convert_fusion.refs_0_, bf16[896,512]{1,0:T(8,128)(2,1)S(1)} %collective-permute-done.15.refs_1_, bf16[896,512]{1,0:T(8,128)(2,1)S(1)} %collective-permute-done.16.refs_2_, ...), custom_call_target="tpu_custom_call", output_to_operand_aliasing={{}: (6, {})} | custom-call | tf_op jit(solution)/shard_map/pallas_call | solution.py:172
  99.5 2.1 %shard_map.63.refs_3_ = f32[3072,512]{1,0:T(8,128)} custom-call(bf16[512,512]{1,0:T(8,128)(2,1)S(1)} %add_convert_fusion.2.refs_0_, bf16[512,512]{1,0:T(8,128)(2,1)S(1)} %collective-permute-done.12.refs_1_, bf16[512,512]{1,0:T(8,128)(2,1)S(1)} %collective-permute-done.13.refs_2_, ...), custom_call_target="tpu_custom_call", output_to_operand_aliasing={{}: (6, {})} | custom-call | tf_op jit(solution)/shard_map/pallas_call | solution.py:172
  101.6 1.2 %shard_map.64.refs_3_ = f32[3072,512]{1,0:T(8,128)} custom-call(bf16[384,512]{1,0:T(8,128)(2,1)S(1)} %collective-permute-done.10.refs_0_, bf16[2048,512]{1,0:T(8,128)(2,1)S(1)} %copy-done, f32[384,512]{1,0:T(8,128)S(1)} %shard_map.59.refs_2_, f32[3072,512]{1,0:T(8,128)} %shard_map.63.refs_3_), custom_call_target="tpu_custom_call", output_to_operand_aliasing={{}: (3, {})} | custom-call | tf_op jit(solution)/shard_map/pallas_call | solution.py:172
  102.8 1.0 shard_map.65.refs_3_
  103.8 1.0 shard_map.66
  (57 shorter events, 2.8 us)
Async XLA Ops:
  1.2 16.5 %copy-start.3 = (f32[512]{0:T(512)S(1)}, f32[512]{0:T(512)}, u32[]{:S(2)}) copy-start(f32[512]{0:T(512)} %param.6) | copy-start | bytes 6148
  1.2 16.6 %copy-start.2 = (f32[512]{0:T(512)S(1)}, f32[512]{0:T(512)}, u32[]{:S(2)}) copy-start(f32[512]{0:T(512)} %param.7) | copy-start | bytes 6148
  4.1 4.6 %collective-permute-start = (f32[2,512]{1,0:T(2,128)S(1)}, f32[2,512]{1,0:T(2,128)S(1)}, u32[]{:S(2)}, u32[]{:S(2)}) collective-permute-start(f32[2,512]{1,0:T(2,128)S(1)} %get-tuple-element.13), channel_id=1, source_target_pairs={{0,4},{4,0},{8,12},{12,8},{16,20},{20,16},{24,28},{28,24},{1,5},{5... | collective-permute-start | bytes 12296 | tf_op jit(solution)/shard_map/ppermute | solution.py:210
  8.8 3.8 %collective-permute-start.1 = (f32[2,512]{1,0:T(2,128)S(1)}, f32[2,512]{1,0:T(2,128)S(1)}, u32[]{:S(2)}, u32[]{:S(2)}) collective-permute-start(f32[2,512]{1,0:T(2,128)S(1)} %pad_maximum_fusion.1), channel_id=1, source_target_pairs={{0,8},{4,12},{8,0},{12,4},{16,24},{20,28},{24,16},{28,20},{1,9},{5... | collective-permute-start | bytes 12296 | tf_op jit(solution)/shard_map/ppermute | solution.py:210
  12.6 5.1 %collective-permute-start.2 = (f32[2,512]{1,0:T(2,128)S(1)}, f32[2,512]{1,0:T(2,128)S(1)}, u32[]{:S(2)}, u32[]{:S(2)}) collective-permute-start(f32[2,512]{1,0:T(2,128)S(1)} %pad_maximum_fusion.2), channel_id=1, source_target_pairs={{0,16},{4,20},{8,24},{12,28},{16,0},{20,4},{24,8},{28,12},{1,17},{... | collective-permute-start | bytes 12296 | tf_op jit(solution)/shard_map/ppermute | solution.py:210
  15.7 34.3 %collective-permute-start.23 = (bf16[256,512]{1,0:T(8,128)(2,1)S(1)}, bf16[256,512]{1,0:T(8,128)(2,1)S(1)}, u32[]{:S(2)}, u32[]{:S(2)}) collective-permute-start(bf16[256,512]{1,0:T(8,128)(2,1)S(1)} %get-tuple-element.16), channel_id=1, source_target_pairs={{0,2},{1,3},{2,0},{3,1},{4,6},{5,7},{6,4},{7,5},{8,10},{9,11},{10,... | collective-permute-start | bytes 786440 | tf_op jit(solution)/shard_map/ppermute | solution.py:193
  17.2 58.2 %collective-permute-start.19 = (bf16[768,512]{1,0:T(8,128)(2,1)S(1)}, bf16[768,512]{1,0:T(8,128)(2,1)S(1)}, u32[]{:S(2)}, u32[]{:S(2)}) collective-permute-start(bf16[768,512]{1,0:T(8,128)(2,1)S(1)} %get-tuple-element.14), channel_id=1, source_target_pairs={{0,2},{1,3},{2,0},{3,1},{4,6},{5,7},{6,4},{7,5},{8,10},{9,11},{10,... | collective-permute-start | bytes 2359304 | tf_op jit(solution)/shard_map/ppermute | solution.py:193
  18.3 25.3 %collective-permute-start.6 = (bf16[128,512]{1,0:T(8,128)(2,1)S(1)}, bf16[128,512]{1,0:T(8,128)(2,1)S(1)}, u32[]{:S(2)}, u32[]{:S(2)}) collective-permute-start(bf16[128,512]{1,0:T(8,128)(2,1)S(1)} %get-tuple-element.17.refs_0_), channel_id=1, source_target_pairs={{0,2},{1,3},{2,0},{3,1},{4,6},{5,7},{6,4},{7,5},{8,10},{9,11},{10,... | collective-permute-start | bytes 393224 | tf_op jit(solution)/shard_map/ppermute | solution.py:193
  19.9 23.8 %collective-permute-start.8 = (bf16[128,512]{1,0:T(8,128)(2,1)S(1)}, bf16[128,512]{1,0:T(8,128)(2,1)S(1)}, u32[]{:S(2)}, u32[]{:S(2)}) collective-permute-start(bf16[128,512]{1,0:T(8,128)(2,1)S(1)} %get-tuple-element.17.refs_0_), channel_id=1, source_target_pairs={{0,1},{1,0},{2,3},{3,2},{4,5},{5,4},{6,7},{7,6},{8,9},{9,8},{10,11... | collective-permute-start | bytes 393224 | tf_op jit(solution)/shard_map/ppermute | solution.py:196
  20.0 22.2 %collective-permute-start.20 = (f32[5,512]{1,0:T(8,128)S(1)}, f32[5,512]{1,0:T(8,128)S(1)}, u32[]{:S(2)}, u32[]{:S(2)}) collective-permute-start(f32[5,512]{1,0:T(8,128)S(1)} %pad_maximum_fusion), channel_id=1, source_target_pairs={{0,2},{1,3},{2,0},{3,1},{4,6},{5,7},{6,4},{7,5},{8,10},{9,11},{10,... | collective-permute-start | bytes 30728 | tf_op jit(solution)/shard_map/ppermute | solution.py:193
  42.2 5.4 %collective-permute-start.3 = (bf16[128,512]{1,0:T(8,128)(2,1)S(1)}, bf16[128,512]{1,0:T(8,128)(2,1)S(1)}, u32[]{:S(2)}, u32[]{:S(2)}) collective-permute-start(bf16[128,512]{1,0:T(8,128)(2,1)S(1)} %get-tuple-element.18.refs_0_), channel_id=1, source_target_pairs={{0,2},{1,3},{2,0},{3,1},{4,6},{5,7},{6,4},{7,5},{8,10},{9,11},{10,... | collective-permute-start | bytes 393224 | tf_op jit(solution)/shard_map/ppermute | solution.py:193
  43.7 3.8 %collective-permute-start.5 = (bf16[128,512]{1,0:T(8,128)(2,1)S(1)}, bf16[128,512]{1,0:T(8,128)(2,1)S(1)}, u32[]{:S(2)}, u32[]{:S(2)}) collective-permute-start(bf16[128,512]{1,0:T(8,128)(2,1)S(1)} %get-tuple-element.18.refs_0_), channel_id=1, source_target_pairs={{0,1},{1,0},{2,3},{3,2},{4,5},{5,4},{6,7},{7,6},{8,9},{9,8},{10,11... | collective-permute-start | bytes 393224 | tf_op jit(solution)/shard_map/ppermute | solution.py:196
  43.7 33.3 %collective-permute-start.16 = (bf16[896,512]{1,0:T(8,128)(2,1)S(1)}, bf16[896,512]{1,0:T(8,128)(2,1)S(1)}, u32[]{:S(2)}, u32[]{:S(2)}) collective-permute-start(bf16[896,512]{1,0:T(8,128)(2,1)S(1)} %add_convert_fusion.refs_0_), channel_id=1, source_target_pairs={{0,2},{1,3},{2,0},{3,1},{4,6},{5,7},{6,4},{7,5},{8,10},{9,11},{10,... | collective-permute-start | bytes 2752520 | tf_op jit(solution)/shard_map/ppermute | solution.py:193
  47.5 4.3 %collective-permute-start.11 = (bf16[384,512]{1,0:T(8,128)(2,1)S(1)}, bf16[384,512]{1,0:T(8,128)(2,1)S(1)}, u32[]{:S(2)}, u32[]{:S(2)}) collective-permute-start(bf16[384,512]{1,0:T(8,128)(2,1)S(1)} %add_convert_fusion.3.refs_0_), channel_id=1, source_target_pairs={{0,1},{1,0},{2,3},{3,2},{4,5},{5,4},{6,7},{7,6},{8,9},{9,8},{10,11... | collective-permute-start | bytes 1179656 | tf_op jit(solution)/shard_map/ppermute | solution.py:196
  47.5 27.7 %collective-permute-start.9 = (bf16[384,512]{1,0:T(8,128)(2,1)S(1)}, bf16[384,512]{1,0:T(8,128)(2,1)S(1)}, u32[]{:S(2)}, u32[]{:S(2)}) collective-permute-start(bf16[384,512]{1,0:T(8,128)(2,1)S(1)} %add_convert_fusion.3.refs_0_), channel_id=1, source_target_pairs={{0,2},{1,3},{2,0},{3,1},{4,6},{5,7},{6,4},{7,5},{8,10},{9,11},{10,... | collective-permute-start | bytes 1179656 | tf_op jit(solution)/shard_map/ppermute | solution.py:193
  50.0 1.5 %collective-permute-start.22 = (bf16[256,512]{1,0:T(8,128)(2,1)S(1)}, bf16[256,512]{1,0:T(8,128)(2,1)S(1)}, u32[]{:S(2)}, u32[]{:S(2)}) collective-permute-start(bf16[256,512]{1,0:T(8,128)(2,1)S(1)} %add_convert_fusion.5.refs_0_), channel_id=1, source_target_pairs={{0,1},{1,0},{2,3},{3,2},{4,5},{5,4},{6,7},{7,6},{8,9},{9,8},{10,11... | collective-permute-start | bytes 786440 | tf_op jit(solution)/shard_map/ppermute | solution.py:196
  50.2 40.6 %copy-start = (bf16[2048,512]{1,0:T(8,128)(2,1)S(1)}, bf16[2048,512]{1,0:T(8,128)(2,1)}, u32[]{:S(2)}) copy-start(bf16[2048,512]{1,0:T(8,128)(2,1)} %refs_1_.5) | copy-start | bytes 6291460
  50.2 40.6 %copy-start.1 = (f32[512]{0:T(512)S(1)}, f32[512]{0:T(512)}, u32[]{:S(2)}) copy-start(f32[512]{0:T(512)} %param.9) | copy-start | bytes 6148
  51.5 38.8 %collective-permute-start.15 = (bf16[896,512]{1,0:T(8,128)(2,1)S(1)}, bf16[896,512]{1,0:T(8,128)(2,1)S(1)}, u32[]{:S(2)}, u32[]{:S(2)}) collective-permute-start(bf16[896,512]{1,0:T(8,128)(2,1)S(1)} %add_convert_fusion.refs_0_), channel_id=1, source_target_pairs={{0,1},{1,0},{2,3},{3,2},{4,5},{5,4},{6,7},{7,6},{8,9},{9,8},{10,11... | collective-permute-start | bytes 2752520 | tf_op jit(solution)/shard_map/ppermute | solution.py:196
  51.8 38.0 %collective-permute-start.18 = (bf16[768,512]{1,0:T(8,128)(2,1)S(1)}, bf16[768,512]{1,0:T(8,128)(2,1)S(1)}, u32[]{:S(2)}, u32[]{:S(2)}) collective-permute-start(bf16[768,512]{1,0:T(8,128)(2,1)S(1)} %add_convert_fusion.1.refs_0_), channel_id=1, source_target_pairs={{0,1},{1,0},{2,3},{3,2},{4,5},{5,4},{6,7},{7,6},{8,9},{9,8},{10,11... | collective-permute-start | bytes 2359304 | tf_op jit(solution)/shard_map/ppermute | solution.py:196
  75.2 2.2 %collective-permute-start.24 = (bf16[256,512]{1,0:T(8,128)(2,1)S(1)}, bf16[256,512]{1,0:T(8,128)(2,1)S(1)}, u32[]{:S(2)}, u32[]{:S(2)}) collective-permute-start(bf16[256,512]{1,0:T(8,128)(2,1)S(1)} %add_convert_fusion.4.refs_2_), channel_id=1, source_target_pairs={{0,1},{1,0},{2,3},{3,2},{4,5},{5,4},{6,7},{7,6},{8,9},{9,8},{10,11... | collective-permute-start | bytes 786440 | tf_op jit(solution)/shard_map/ppermute | solution.py:196
  75.4 14.4 %collective-permute-start.13 = (bf16[512,512]{1,0:T(8,128)(2,1)S(1)}, bf16[512,512]{1,0:T(8,128)(2,1)S(1)}, u32[]{:S(2)}, u32[]{:S(2)}) collective-permute-start(bf16[512,512]{1,0:T(8,128)(2,1)S(1)} %add_convert_fusion.2.refs_0_), channel_id=1, source_target_pairs={{0,2},{1,3},{2,0},{3,1},{4,6},{5,7},{6,4},{7,5},{8,10},{9,11},{10,... | collective-permute-start | bytes 1572872 | tf_op jit(solution)/shard_map/ppermute | solution.py:193
  77.0 13.8 %collective-permute-start.17 = (bf16[896,512]{1,0:T(8,128)(2,1)S(1)}, bf16[896,512]{1,0:T(8,128)(2,1)S(1)}, u32[]{:S(2)}, u32[]{:S(2)}) collective-permute-start(bf16[896,512]{1,0:T(8,128)(2,1)S(1)} %collective-permute-done.16.refs_2_), channel_id=1, source_target_pairs={{0,1},{1,0},{2,3},{3,2},{4,5},{5,4},{6,7},{7,6},{8,9},{9,8},{10,11... | collective-permute-start | bytes 2752520 | tf_op jit(solution)/shard_map/ppermute | solution.py:196
  77.4 13.0 %collective-permute-start.21 = (bf16[768,512]{1,0:T(8,128)(2,1)S(1)}, bf16[768,512]{1,0:T(8,128)(2,1)S(1)}, u32[]{:S(2)}, u32[]{:S(2)}) collective-permute-start(bf16[768,512]{1,0:T(8,128)(2,1)S(1)} %fusion.refs_2_), channel_id=1, source_target_pairs={{0,1},{1,0},{2,3},{3,2},{4,5},{5,4},{6,7},{7,6},{8,9},{9,8},{10,11... | collective-permute-start | bytes 2359304 | tf_op jit(solution)/shard_map/ppermute | solution.py:196
  89.8 9.7 %collective-permute-start.12 = (bf16[512,512]{1,0:T(8,128)(2,1)S(1)}, bf16[512,512]{1,0:T(8,128)(2,1)S(1)}, u32[]{:S(2)}, u32[]{:S(2)}) collective-permute-start(bf16[512,512]{1,0:T(8,128)(2,1)S(1)} %add_convert_fusion.2.refs_0_), channel_id=1, source_target_pairs={{0,1},{1,0},{2,3},{3,2},{4,5},{5,4},{6,7},{7,6},{8,9},{9,8},{10,11... | collective-permute-start | bytes 1572872 | tf_op jit(solution)/shard_map/ppermute | solution.py:196
  89.8 9.7 %collective-permute-start.14 = (bf16[512,512]{1,0:T(8,128)(2,1)S(1)}, bf16[512,512]{1,0:T(8,128)(2,1)S(1)}, u32[]{:S(2)}, u32[]{:S(2)}) collective-permute-start(bf16[512,512]{1,0:T(8,128)(2,1)S(1)} %collective-permute-done.13.refs_2_), channel_id=1, source_target_pairs={{0,1},{1,0},{2,3},{3,2},{4,5},{5,4},{6,7},{7,6},{8,9},{9,8},{10,11... | collective-permute-start | bytes 1572872 | tf_op jit(solution)/shard_map/ppermute | solution.py:196
  90.3 11.3 %collective-permute-start.10 = (bf16[384,512]{1,0:T(8,128)(2,1)S(1)}, bf16[384,512]{1,0:T(8,128)(2,1)S(1)}, u32[]{:S(2)}, u32[]{:S(2)}) collective-permute-start(bf16[384,512]{1,0:T(8,128)(2,1)S(1)} %collective-permute-done.9.refs_2_), channel_id=1, source_target_pairs={{0,1},{1,0},{2,3},{3,2},{4,5},{5,4},{6,7},{7,6},{8,9},{9,8},{10,11... | collective-permute-start | bytes 1179656 | tf_op jit(solution)/shard_map/ppermute | solution.py:196
  90.4 12.4 %collective-permute-start.7 = (bf16[128,512]{1,0:T(8,128)(2,1)S(1)}, bf16[128,512]{1,0:T(8,128)(2,1)S(1)}, u32[]{:S(2)}, u32[]{:S(2)}) collective-permute-start(bf16[128,512]{1,0:T(8,128)(2,1)S(1)} %collective-permute-done.6.refs_2_), channel_id=1, source_target_pairs={{0,1},{1,0},{2,3},{3,2},{4,5},{5,4},{6,7},{7,6},{8,9},{9,8},{10,11... | collective-permute-start | bytes 393224 | tf_op jit(solution)/shard_map/ppermute | solution.py:196
  90.8 12.9 %collective-permute-start.4 = (bf16[128,512]{1,0:T(8,128)(2,1)S(1)}, bf16[128,512]{1,0:T(8,128)(2,1)S(1)}, u32[]{:S(2)}, u32[]{:S(2)}) collective-permute-start(bf16[128,512]{1,0:T(8,128)(2,1)S(1)} %collective-permute-done.3.refs_2_), channel_id=1, source_target_pairs={{0,1},{1,0},{2,3},{3,2},{4,5},{5,4},{6,7},{7,6},{8,9},{9,8},{10,11... | collective-permute-start | bytes 393224 | tf_op jit(solution)/shard_map/ppermute | solution.py:196
